TPU v7x, 32 devices: a whole 2x2x4 slice. The times are simulated.
32 devices in a mesh: gx: 8 (over y, x, core), gy: 4 (over z).
Axes of the slice: x: 2, y: 2, z: 4, core: 2. Of those that a mesh axis runs over, the one named last changes fastest.
Arguments:
- layer_early: bfloat16 [1024, 8192], P(None, ('gx', 'gy')), may hold values from -48 to 48
- layer_late: bfloat16 [1024, 8192], P(('gx', 'gy')), may hold values from -48 to 48
Outputs:
- similarity: float32 [], replicated
- token_share: float32 [1024], P(('gx', 'gy'))
- early_rows: bfloat16 [1024, 8192], P(('gx', 'gy'))
- late_rows: bfloat16 [1024, 8192], P(('gx', 'gy'))
All inputs are finite; a program needn't handle non-finite values.
Results may differ from a plain program's by a relative error of at most 0.0015.
Values may be sent and summed in bfloat16 or wider, within the bound.
A program may use at most 128 MiB of HBM per device.

v0:
```python
import jax
import jax.numpy as jnp
from jax import lax
from jax.sharding import PartitionSpec as P


def pair_terms(left_early, left_late, right_early, right_late):
    dims = (((1,), (1,)), ((), ()))
    block_early = lax.dot_general(left_early, right_early, dims, preferred_element_type=jnp.float32)
    block_late = lax.dot_general(left_late, right_late, dims, preferred_element_type=jnp.float32)
    return (
        jnp.sum(block_early * block_late, axis=1),
        jnp.sum(block_early * block_early),
        jnp.sum(block_late * block_late),
    )


def body(layer_early, layer_late):
    total_rows = layer_early.shape[0]
    early_values = layer_early.astype(jnp.float32)
    early_cols = (early_values - jnp.mean(early_values, axis=0)).astype(jnp.bfloat16)
    late_values = layer_late.astype(jnp.float32)
    column_sums = lax.psum(jnp.sum(late_values, axis=0), ("gx", "gy"))
    late_rows = (late_values - column_sums / total_rows).astype(jnp.bfloat16)
    early_rows = lax.all_to_all(early_cols, ("gx", "gy"), split_axis=0, concat_axis=1, tiled=True)
    block_early, block_late = (
        lax.all_gather(early_rows, "gy", axis=0, tiled=True),
        lax.all_gather(late_rows, "gy", axis=0, tiled=True),
    )
    row_part, early_part, late_part = pair_terms(
        block_early,
        block_late,
        lax.all_gather(early_rows, "gx", axis=0, tiled=True),
        lax.all_gather(late_rows, "gx", axis=0, tiled=True),
    )
    own_align = lax.psum_scatter(row_part, "gy", scatter_dimension=0, tiled=True)
    total_kl, total_kk, total_ll = lax.psum(
        (jnp.sum(row_part), early_part, late_part), ("gx", "gy")
    )
    scale_norm = jnp.sqrt(total_kk * total_ll)
    similarity = total_kl / scale_norm
    token_share = total_rows * own_align / scale_norm
    return (similarity, token_share, early_rows, late_rows)


def solution(mesh):
    in_specs = (P(None, ("gx", "gy")), P(("gx", "gy"), None))
    out_specs = (P(), P(("gx", "gy")), P(("gx", "gy"), None), P(("gx", "gy"), None))
    return jax.shard_map(body, mesh=mesh, in_specs=in_specs, out_specs=out_specs, check_vma=False)
```

profile of v0, /device:TPU:0, one launch (start us, length us, event | category | flops | bytes accessed | tf_op | source)
XLA Modules:
  0.0 298.2 jit_solution(8457581897998979989)
XLA Ops:
  7.2 0.0 all-gather.9.cloned.1.call-start
  7.2 1.2 convert_reduce_fusion
  8.4 42.1 %psum.28 = f32[8192]{0:T(1024)S(1)} all-reduce(f32[8192]{0:T(1024)S(1)} %convert_reduce_fusion), channel_id=1, replica_groups=mesh['gx'=8,'gy'=4] {'gx','gy'}, use_global_device_ids=true, to_apply=%region_2.0 | all-reduce | flops 8192 | bytes 65536 | tf_op jit(solution)/shard_map/psum | solution.py:23
  50.6 1.9 fusion.1
  52.5 0.0 all-gather.11.cloned.1.call-start
  52.5 0.7 all-gather.11.cloned.1.call-update
  53.3 0.0 all-gather.5.cloned.1.call-start
  53.3 1.2 convert_reduce_fusion.1
  54.5 1.1 fusion
  55.6 28.2 %all_to_all.19 = bf16[32,32,256]{2,1,0:T(8,128)(2,1)S(1)} all-to-all(bf16[32,32,256]{2,1,0:T(8,128)(2,1)S(1)} %bitcast.12), channel_id=1, replica_groups=mesh['gx'=8,'gy'=4] {'gx','gy'}, dimensions={0} | all-to-all | bytes 1048576 | tf_op jit(solution)/shard_map/all_to_all | solution.py:25
  83.9 0.8 copy.8
  84.7 0.0 all-gather.5.cloned.1.call-update
  84.7 0.0 all-gather.7.cloned.1.call-start
  84.8 0.5 all-gather.7.cloned.1.call-update
  85.3 0.6 dynamic-slice
  86.6 22.4 %all-gather.9.cloned.1.call-done = bf16[128,8192]{1,0:T(8,128)(2,1)} async-done(((bf16[32,8192]{1,0:T(8,128)(2,1)}), bf16[128,8192]{1,0:T(8,128)(2,1)}) %all-gather.9.cloned.1.call-update) | async-done | bytes 2097168 | tf_op jit(solution)/shard_map/all_gather | solution.py:28
  109.0 38.1 %all-gather.11.cloned.1.call-done = bf16[256,8192]{1,0:T(8,128)(2,1)} async-done(((bf16[32,8192]{1,0:T(8,128)(2,1)}), bf16[256,8192]{1,0:T(8,128)(2,1)}) %all-gather.11.cloned.1.call-update) | async-done | bytes 4194320 | tf_op jit(solution)/shard_map/all_gather | solution.py:34
  147.1 4.4 %fusion.3 = f32[128,256]{1,0:T(8,128)S(1)} fusion(bf16[128,8192]{1,0:T(8,128)(2,1)} %all-gather.9.cloned.1.call-done, bf16[256,8192]{1,0:T(8,128)(2,1)} %all-gather.11.cloned.1.call-done), kind=kOutput, calls=%fused_computation.14 | convolution fusion | flops 536870912 | bytes 6422528 | tf_op jit(solution)/shard_map/dot_general | solution.py:10
  151.5 43.5 %all-gather.5.cloned.1.call-done = bf16[128,8192]{1,0:T(8,128)(2,1)} async-done(((bf16[32,8192]{1,0:T(8,128)(2,1)}), bf16[128,8192]{1,0:T(8,128)(2,1)}) %all-gather.5.cloned.1.call-update) | async-done | bytes 2097168 | tf_op jit(solution)/shard_map/all_gather | solution.py:27
  195.0 37.7 %all-gather.7.cloned.1.call-done = bf16[256,8192]{1,0:T(8,128)(2,1)} async-done(((bf16[32,8192]{1,0:T(8,128)(2,1)}), bf16[256,8192]{1,0:T(8,128)(2,1)}) %all-gather.7.cloned.1.call-update) | async-done | bytes 4194320 | tf_op jit(solution)/shard_map/all_gather | solution.py:33
  232.7 5.0 %multiply_reduce_fusion.2 = (f32[128]{0:T(128)S(1)}, f32[]{:T(128)}, f32[]{:T(128)}, f32[]{:T(128)}) fusion(f32[128,256]{1,0:T(8,128)S(1)} %fusion.3, bf16[128,8192]{1,0:T(8,128)(2,1)} %all-gather.5.cloned.1.call-done, bf16[256,8192]{1,0:T(8,128)(2,1)} %all-gather.7.cloned.1.call-done), kind=kOutput, calls=%fused_computation.8 | convolution fusion | flops 537100160 | bytes 6423052 | tf_op jit(solution)/shard_map/dot_general | solution.py:9
  237.7 39.6 %all-reduce.1 = (f32[]{:T(128)}, f32[]{:T(128)}, f32[]{:T(128)}) all-reduce(f32[]{:T(128)} %get-tuple-element.5, f32[]{:T(128)} %get-tuple-element.7, f32[]{:T(128)} %get-tuple-element.6), channel_id=1, replica_groups=mesh['gx'=8,'gy'=4] {'gx','gy'}, use_global_device_ids=true, to_apply=%region_4.0 | all-reduce | flops 3 | bytes 24 | tf_op jit(solution)/shard_map/psum | solution.py:37
  278.7 10.6 %all-reduce = f32[128]{0:T(128)S(1)} all-reduce(f32[128]{0:T(128)S(1)} %get-tuple-element.4), channel_id=2, replica_groups=mesh['gx'=8,'gy'=4] {'gy'}, use_global_device_ids=true, to_apply=%region_10.0.clone | all-reduce | flops 128 | bytes 1024
  290.0 0.6 fusion.2
  (5 shorter events, 0.0 us)
Async XLA Ops:
  7.2 78.2 %copy-start = (u32[32]{0:T(128)S(1)}, u32[32]{0:T(128)}, u32[]{:S(2)}) copy-start(u32[32]{0:T(128)} %constant.11) | copy-start | bytes 388
  7.2 101.8 %all-gather.9.cloned.1.call-start = ((), (), s32[]{:S(2)}) async-start(), calls=%async_computation.3 | async-start | bytes 2621440 | tf_op jit(solution)/shard_map/all_gather | solution.py:28
  52.5 94.6 %all-gather.11.cloned.1.call-start = ((), (), s32[]{:S(2)}) async-start(), calls=%async_computation.4 | async-start | bytes 4718592 | tf_op jit(solution)/shard_map/all_gather | solution.py:34
  53.3 141.7 %all-gather.5.cloned.1.call-start = ((), (), s32[]{:S(2)}) async-start(), calls=%async_computation.1 | async-start | bytes 2621440 | tf_op jit(solution)/shard_map/all_gather | solution.py:27
  84.7 147.9 %all-gather.7.cloned.1.call-start = ((), (), s32[]{:S(2)}) async-start(), calls=%async_computation.2 | async-start | bytes 4718592 | tf_op jit(solution)/shard_map/all_gather | solution.py:33
Sparse Core Ops, SparseCore 0:
  52.6 56.3 all-gather.8
  111.5 35.5 all-gather.10
  149.3 45.6 all-gather.4
  197.3 35.3 all-gather.6
where the time goes:
time: 299 us; the launch traced here: 298 us
  waiting for transfers between devices  143 us (48%)
  blocking collectives  121 us (40%)
  between operations  17.6 us (6%)
  matrix products  9.4 us (3%)
  other arithmetic  6.03 us (2%)
    all_gather x1, waiting for transfers between devices, body(): lax.all_gather(early_rows, 'gy', axis=0, tiled=True)  43.5 us
    psum x1, blocking collectives, body(): column_sums = lax.psum(jnp.sum(late_values, axis=0), ('gx', 'gy'))  42.1 us
    psum x1, blocking collectives, body(): lax.psum((jnp.sum(row_part), early_part, late_part), ('gx', 'gy'))  39.6 us
    all_gather x1, waiting for transfers between devices, body(): lax.all_gather(late_rows, 'gx', axis=0, tiled=True)  38.1 us
    all_gather x1, waiting for transfers between devices, body(): lax.all_gather(early_rows, 'gx', axis=0, tiled=True)  37.7 us
    all_to_all x1, blocking collectives, body(): lax.all_to_all(early_cols, ('gx', 'gy'), split_axis=0, concat_axis=1, til...  28.2 us
    all_gather x1, waiting for transfers between devices, body(): lax.all_gather(late_rows, 'gy', axis=0, tiled=True)  22.4 us
    unnamed x1, blocking collectives  10.6 us
  transfers between devices with their start and end apart: 4, of which 4 were waited for; matrix products, arithmetic and copies ran while one was open for 3% of the time, Pallas kernels for 0%

commit v1 on v0

--- a/solution.py
+++ b/solution.py
@@ -20,7 +20,9 @@
     early_values = layer_early.astype(jnp.float32)
     early_cols = (early_values - jnp.mean(early_values, axis=0)).astype(jnp.bfloat16)
     late_values = layer_late.astype(jnp.float32)
-    column_sums = lax.psum(jnp.sum(late_values, axis=0), ("gx", "gy"))
+    column_sums = jnp.sum(late_values, axis=0)
+    for mesh_axis in ("gx", "gy"):
+        column_sums = lax.psum(column_sums, mesh_axis)
     late_rows = (late_values - column_sums / total_rows).astype(jnp.bfloat16)
     early_rows = lax.all_to_all(early_cols, ("gx", "gy"), split_axis=0, concat_axis=1, tiled=True)
     block_early, block_late = (

time: 299 us -> 298 us (level)
  waiting for transfers between devices: 143 us -> 138 us
  blocking collectives: 121 us -> 125 us
    all_gather x1, waiting for transfers between devices: 22.4 us -> 17.8 us  [body(): lax.all_gather(late_rows, 'gy', axis=0, tiled=True)]
    psum x1 -> x2, blocking collectives: 42.1 us -> 44.8 us  [body(): column_sums = lax.psum(column_sums, mesh_axis)]
where the time goes in v1:
time: 298 us; the launch traced here: 297 us
  waiting for transfers between devices  138 us (46%)
  blocking collectives  125 us (42%)
  between operations  17.6 us (6%)
  matrix products  9.4 us (3%)
  other arithmetic  6.06 us (2%)
    psum x2, blocking collectives, body(): column_sums = lax.psum(column_sums, mesh_axis)  44.8 us
    all_gather x1, waiting for transfers between devices, body(): lax.all_gather(early_rows, 'gy', axis=0, tiled=True)  43.5 us
    psum x1, blocking collectives, body(): lax.psum((jnp.sum(row_part), early_part, late_part), ('gx', 'gy'))  39.6 us
    all_gather x1, waiting for transfers between devices, body(): lax.all_gather(late_rows, 'gx', axis=0, tiled=True)  37.8 us
    all_gather x1, waiting for transfers between devices, body(): lax.all_gather(early_rows, 'gx', axis=0, tiled=True)  37.7 us
    all_to_all x1, blocking collectives, body(): lax.all_to_all(early_cols, ('gx', 'gy'), split_axis=0, concat_axis=1, til...  29.7 us
    all_gather x1, waiting for transfers between devices, body(): lax.all_gather(late_rows, 'gy', axis=0, tiled=True)  17.8 us
    unnamed x1, blocking collectives  10.6 us
  transfers between devices with their start and end apart: 4, of which 4 were waited for; matrix products, arithmetic and copies ran while one was open for 3% of the time, Pallas kernels for 0%

profile of v1, /device:TPU:0, one launch (start us, length us, event | category | flops | bytes accessed | tf_op | source)
XLA Modules:
  0.0 297.4 jit_solution(12857150651782097719)
XLA Ops:
  7.2 0.0 all-gather.9.cloned.1.call-start
  7.2 1.2 convert_reduce_fusion
  8.4 25.5 %psum.35 = f32[8192]{0:T(1024)S(1)} all-reduce(f32[8192]{0:T(1024)S(1)} %convert_reduce_fusion), channel_id=1, replica_groups=mesh['gx'=8,'gy'=4] {'gx'}, use_global_device_ids=true, to_apply=%region_2.0 | all-reduce | flops 8192 | bytes 65536 | tf_op jit(solution)/shard_map/psum | solution.py:25
  33.9 19.2 %psum.36 = f32[8192]{0:T(1024)S(1)} all-reduce(f32[8192]{0:T(1024)S(1)} %psum.35), channel_id=1, replica_groups=mesh['gx'=8,'gy'=4] {'gy'}, use_global_device_ids=true, to_apply=%region_3.0 | all-reduce | flops 8192 | bytes 65536 | tf_op jit(solution)/shard_map/psum | solution.py:25
  53.2 1.9 fusion.1
  55.2 0.0 all-gather.11.cloned.1.call-start
  55.2 0.7 all-gather.11.cloned.1.call-update
  55.9 0.0 all-gather.5.cloned.1.call-start
  56.0 1.2 convert_reduce_fusion.1
  57.2 1.2 fusion
  58.3 29.7 %all_to_all.19 = bf16[32,32,256]{2,1,0:T(8,128)(2,1)S(1)} all-to-all(bf16[32,32,256]{2,1,0:T(8,128)(2,1)S(1)} %bitcast.12), channel_id=1, replica_groups=mesh['gx'=8,'gy'=4] {'gx','gy'}, dimensions={0} | all-to-all | bytes 1048576 | tf_op jit(solution)/shard_map/all_to_all | solution.py:27
  88.1 0.8 copy.8
  88.9 0.0 all-gather.7.cloned.1.call-start
  89.0 0.5 all-gather.7.cloned.1.call-update
  89.5 0.6 dynamic-slice
  90.8 17.8 %all-gather.9.cloned.1.call-done = bf16[128,8192]{1,0:T(8,128)(2,1)} async-done(((bf16[32,8192]{1,0:T(8,128)(2,1)}), bf16[128,8192]{1,0:T(8,128)(2,1)}) %all-gather.9.cloned.1.call-update) | async-done | bytes 2097168 | tf_op jit(solution)/shard_map/all_gather | solution.py:30
  108.6 37.8 %all-gather.11.cloned.1.call-done = bf16[256,8192]{1,0:T(8,128)(2,1)} async-done(((bf16[32,8192]{1,0:T(8,128)(2,1)}), bf16[256,8192]{1,0:T(8,128)(2,1)}) %all-gather.11.cloned.1.call-update) | async-done | bytes 4194320 | tf_op jit(solution)/shard_map/all_gather | solution.py:36
  146.3 4.4 %fusion.3 = f32[128,256]{1,0:T(8,128)S(1)} fusion(bf16[128,8192]{1,0:T(8,128)(2,1)} %all-gather.9.cloned.1.call-done, bf16[256,8192]{1,0:T(8,128)(2,1)} %all-gather.11.cloned.1.call-done), kind=kOutput, calls=%fused_computation.14 | convolution fusion | flops 536870912 | bytes 6422528 | tf_op jit(solution)/shard_map/dot_general | solution.py:10
  150.7 43.5 %all-gather.5.cloned.1.call-done = bf16[128,8192]{1,0:T(8,128)(2,1)} async-done(((bf16[32,8192]{1,0:T(8,128)(2,1)}), bf16[128,8192]{1,0:T(8,128)(2,1)}) %all-gather.5.cloned.1.call-update) | async-done | bytes 2097168 | tf_op jit(solution)/shard_map/all_gather | solution.py:29
  194.2 37.7 %all-gather.7.cloned.1.call-done = bf16[256,8192]{1,0:T(8,128)(2,1)} async-done(((bf16[32,8192]{1,0:T(8,128)(2,1)}), bf16[256,8192]{1,0:T(8,128)(2,1)}) %all-gather.7.cloned.1.call-update) | async-done | bytes 4194320 | tf_op jit(solution)/shard_map/all_gather | solution.py:35
  231.9 5.0 %multiply_reduce_fusion.2 = (f32[128]{0:T(128)S(1)}, f32[]{:T(128)}, f32[]{:T(128)}, f32[]{:T(128)}) fusion(f32[128,256]{1,0:T(8,128)S(1)} %fusion.3, bf16[128,8192]{1,0:T(8,128)(2,1)} %all-gather.5.cloned.1.call-done, bf16[256,8192]{1,0:T(8,128)(2,1)} %all-gather.7.cloned.1.call-done), kind=kOutput, calls=%fused_computation.8 | convolution fusion | flops 537100160 | bytes 6423052 | tf_op jit(solution)/shard_map/dot_general | solution.py:9
  236.9 39.6 %all-reduce.1 = (f32[]{:T(128)}, f32[]{:T(128)}, f32[]{:T(128)}) all-reduce(f32[]{:T(128)} %get-tuple-element.5, f32[]{:T(128)} %get-tuple-element.7, f32[]{:T(128)} %get-tuple-element.6), channel_id=1, replica_groups=mesh['gx'=8,'gy'=4] {'gx','gy'}, use_global_device_ids=true, to_apply=%region_5.0 | all-reduce | flops 3 | bytes 24 | tf_op jit(solution)/shard_map/psum | solution.py:39
  277.9 10.6 %all-reduce = f32[128]{0:T(128)S(1)} all-reduce(f32[128]{0:T(128)S(1)} %get-tuple-element.4), channel_id=2, replica_groups=mesh['gx'=8,'gy'=4] {'gy'}, use_global_device_ids=true, to_apply=%region_11.0.clone | all-reduce | flops 128 | bytes 1024
  289.2 0.6 fusion.2
  (6 shorter events, 0.1 us)
Async XLA Ops:
  7.2 82.4 %copy-start = (u32[32]{0:T(128)S(1)}, u32[32]{0:T(128)}, u32[]{:S(2)}) copy-start(u32[32]{0:T(128)} %constant.11) | copy-start | bytes 388
  7.2 101.4 %all-gather.9.cloned.1.call-start = ((), (), s32[]{:S(2)}) async-start(), calls=%async_computation.3 | async-start | bytes 2621440 | tf_op jit(solution)/shard_map/all_gather | solution.py:30
  55.2 91.2 %all-gather.11.cloned.1.call-start = ((), (), s32[]{:S(2)}) async-start(), calls=%async_computation.4 | async-start | bytes 4718592 | tf_op jit(solution)/shard_map/all_gather | solution.py:36
  55.9 138.2 %all-gather.5.cloned.1.call-start = ((), (), s32[]{:S(2)}) async-start(), calls=%async_computation.1 | async-start | bytes 2621440 | tf_op jit(solution)/shard_map/all_gather | solution.py:29
  88.9 143.0 %all-gather.7.cloned.1.call-start = ((), (), s32[]{:S(2)}) async-start(), calls=%async_computation.2 | async-start | bytes 4718592 | tf_op jit(solution)/shard_map/all_gather | solution.py:35
Sparse Core Ops, SparseCore 0:
  55.3 53.2 all-gather.8
  111.0 35.2 all-gather.10
  148.5 45.6 all-gather.4
  196.5 35.3 all-gather.6
